TPU v7x, 8 devices: a whole 2x2x1 slice. The times are simulated.
8 devices in a mesh: dp: 2 (over z, y), cp: 4 (over x, core).
Axes of the slice: x: 2, y: 2, z: 1, core: 2. Of those that a mesh axis runs over, the one named last changes fastest.
Arguments:
- hidden_states: bfloat16 [2, 8192, 896], P('dp', 'cp')
- norm_gain: float32 [896], replicated
- w_gate: bfloat16 [896, 4864], replicated
- w_up: bfloat16 [896, 4864], replicated
- w_down: bfloat16 [4864, 896], replicated
- final_gain: float32 [896], replicated
- w_value: float32 [896], replicated
- b_value: float32 [], replicated
- rewards: float32 [2, 8192], P('dp', 'cp')
- mask: int32 [2, 8192], P('dp', 'cp')
Outputs:
- output 1: float32 [2, 8192], P('dp', 'cp')
- output 2: float32 [2, 8192], P('dp', 'cp')
- output 3: float32 [2, 8192], P('dp', 'cp')
All inputs are finite; a program needn't handle non-finite values.
Results may differ from a plain program's by a relative error of at most 0.001.
Values sent between devices are 32-bit elements.
A program may use at most 1 GiB of HBM per device.

v0:
```python
import math
import jax
import jax.numpy as jnp
from jax import lax
from jax.sharding import PartitionSpec as P

NORM_EPS = 1e-6
WHITEN_EPS = 1e-8
DISCOUNT = 1.0
GAE_LAMBDA = 0.995
LOG_DECAY = math.log(DISCOUNT * GAE_LAMBDA)


def critic_values(x_blk, norm_gain, w_gate, w_up, w_down, final_gain, w_value, b_value):
    x_f32 = x_blk.astype(jnp.float32)
    normed = (x_f32 * lax.rsqrt(jnp.mean(x_f32 * x_f32, axis=-1, keepdims=True) + NORM_EPS) * norm_gain).astype(jnp.bfloat16)
    gate = jnp.einsum('bsd,df->bsf', normed, w_gate, preferred_element_type=jnp.float32)
    up_val = jnp.einsum('bsd,df->bsf', normed, w_up, preferred_element_type=jnp.float32)
    hidden = (jax.nn.silu(gate) * up_val).astype(jnp.bfloat16)
    resid = x_f32 + jnp.einsum('bsf,fd->bsd', hidden, w_down, preferred_element_type=jnp.float32)
    resid_n = resid * lax.rsqrt(jnp.mean(resid * resid, axis=-1, keepdims=True) + NORM_EPS)
    return jnp.sum(resid_n * (final_gain * w_value), axis=-1) + b_value


def decay_matrix(seq_len):
    positions = jnp.arange(seq_len)
    gap = positions[:, None] - positions[None, :]
    return jnp.where(gap >= 0, jnp.exp(jnp.maximum(gap, 0).astype(jnp.float32) * LOG_DECAY), 0.0)


def tail_decay(seq_len):
    positions = jnp.arange(seq_len)
    return jnp.exp((seq_len - positions).astype(jnp.float32) * LOG_DECAY)


def solution(mesh):
    cp_size = mesh.shape['cp']
    left_perm = [(source, source - 1) for source in range(1, cp_size)]

    def local_step(x_blk, norm_gain, w_gate, w_up, w_down, final_gain, w_value, b_value, rew_blk, mask_blk):
        row_count, seq_len = rew_blk.shape
        mask_f = mask_blk.astype(jnp.float32)
        values = mask_f * critic_values(x_blk, norm_gain, w_gate, w_up, w_down, final_gain, w_value, b_value)
        next_first = lax.ppermute(values[:, 0], 'cp', left_perm)
        next_vals = jnp.concatenate([values[:, 1:], next_first[:, None]], axis=1)
        delta = mask_f * rew_blk + DISCOUNT * next_vals - values
        local_adv = jnp.dot(delta, decay_matrix(seq_len), precision=lax.Precision.HIGHEST)
        head_adv = local_adv[:, 0]
        piece_gain = math.exp(seq_len * LOG_DECAY)

        def carry_step(step_idx, carry):
            return lax.ppermute(head_adv + piece_gain * carry, 'cp', left_perm)

        carry_in = lax.fori_loop(0, cp_size - 1, carry_step, jnp.zeros((row_count,), jnp.float32))
        advantage = local_adv + carry_in[:, None] * tail_decay(seq_len)[None, :]
        local_sums = jnp.stack([jnp.sum(mask_f), jnp.sum(mask_f * advantage), jnp.sum(mask_f * advantage * advantage)])
        totals = lax.psum(local_sums, ('dp', 'cp'))
        mean_adv = totals[1] / totals[0]
        var_adv = totals[2] / totals[0] - mean_adv * mean_adv
        white = mask_f * (advantage - mean_adv) * lax.rsqrt(var_adv + WHITEN_EPS)
        return values, mask_f * (advantage + values), white

    tok_spec = P('dp', 'cp')
    in_specs = (P('dp', 'cp', None), P(None), P(None, None), P(None, None), P(None, None), P(None), P(None), P(), tok_spec, tok_spec)
    return jax.shard_map(local_step, mesh=mesh, in_specs=in_specs, out_specs=(tok_spec, tok_spec, tok_spec), check_vma=False)
```

profile of v0, /device:TPU:0, one launch (start us, length us, event | category | flops | bytes accessed | tf_op | source)
XLA Modules:
  0.0 169.9 jit_solution(9580231293345323384)
XLA Ops:
  0.6 0.0 copy-start.5
  0.6 6.1 %copy.13 = bf16[1,2048,896]{1,2,0:T(8,128)(2,1)} copy(bf16[1,2048,896]{2,1,0:T(8,128)(2,1)} %param.12) | data formatting | bytes 7340032 | tf_op args[0]
  6.8 2.8 %fusion.13 = f32[2048]{0:T(1024)S(1)} fusion(bf16[1,2048,896]{1,2,0:T(8,128)(2,1)} %copy.13), kind=kLoop, calls=%fused_computation.17 | loop fusion | flops 5502976 | bytes 3678208 | tf_op jit(solution)/shard_map/reduce_sum | solution.py:16
  9.6 0.0 copy-done.5
  9.6 29.5 %fusion.19 = f32[2048,4864]{1,0:T(8,128)} fusion(bf16[896,4864]{1,0:T(8,128)(2,1)} %param.14, bf16[1,2048,896]{1,2,0:T(8,128)(2,1)} %copy.13, f32[896]{0:T(1024)S(1)} %copy-done.5, f32[2048]{0:T(1024)S(1)} %add_rsqrt_fusion.1), kind=kOutput, calls=%fused_computation.23 | convolution fusion | flops 17858297856 | bytes 52243968 | tf_op jit(solution)/shard_map/bsd,df->bsf/dot_general | solution.py:17
  39.1 36.5 %multiply_convert_fusion.clone.1.clone.4 = bf16[2048,4864]{1,0:T(8,128)(2,1)} fusion(f32[2048,4864]{1,0:T(8,128)} %fusion.19, bf16[896,4864]{1,0:T(8,128)(2,1)} %param.15, bf16[1,2048,896]{1,2,0:T(8,128)(2,1)} %copy.13, f32[896]{0:T(1024)S(1)} %copy-done.5, f32[2048]{0:T(1024)S(1)} %add_rsqrt_fusion.1), kind=kOutput, calls=%fused_computation.clone.clone.clone.clone.clone.1 | convolution fusion | flops 17918066688 | bytes 72166912 | tf_op jit(solution)/shard_map/bsd,df->bsf/dot_general | solution.py:18
  75.6 0.0 copy-start.2
  75.7 0.0 copy-start.3
  75.7 25.6 %multiply_reduce_fusion.1 = (f32[2048]{0:T(1024)S(1)}, f32[2048,896]{0,1:T(8,128)}) fusion(bf16[1,2048,896]{1,2,0:T(8,128)(2,1)} %copy.13, bf16[4864,896]{1,0:T(8,128)(2,1)} %param.16, bf16[2048,4864]{1,0:T(8,128)(2,1)} %multiply_convert_fusion.clone.1.clone.4), kind=kOutput, calls=%fused_computation.21 | convolution fusion | flops 17858295808 | bytes 39657472 | tf_op jit(solution)/shard_map/bsf,fd->bsd/dot_general | solution.py:20
  101.2 0.0 copy-start
  101.2 0.0 copy-start.4
  101.9 0.0 copy-done.2
  101.9 0.0 copy-done.3
  101.9 5.4 %multiply_reduce_fusion = f32[2048]{0:T(1024)S(1)} fusion(f32[2048,896]{0,1:T(8,128)} %get-tuple-element.35, bf16[1,2048,896]{1,2,0:T(8,128)(2,1)} %copy.13, f32[896]{0:T(1024)S(1)} %mul.114, f32[2048]{0:T(1024)S(1)} %add_rsqrt_fusion), kind=kLoop, calls=%fused_computation.20 | loop fusion | flops 9172992 | bytes 11030016 | tf_op jit(solution)/shard_map/reduce_sum | solution.py:22
  107.3 0.0 copy-done
  107.3 0.0 copy-start.1
  107.4 0.5 slice.26
  107.9 1.3 collective-permute-start.1
  109.2 0.1 slice.25
  109.2 2.0 %collective-permute-done.1 = f32[1]{0:T(128)} collective-permute-done((f32[1]{0:T(128)}, f32[1]{0:T(128)}, u32[]{:S(2)}, u32[]{:S(2)}) %collective-permute-start.1) | collective-permute-done | bytes 36 | tf_op jit(solution)/shard_map/ppermute | solution.py:44
  111.2 0.0 copy-done.4
  111.2 7.4 %fusion.2 = f32[1,2048]{1,0:T(1,128)S(1)} fusion(f32[1,2048]{1,0:T(1,128)S(1)} %convert_multiply_fusion.3, f32[1,1]{1,0:T(1,128)} %bitcast.4, f32[1,2047]{1,0:T(1,128)S(1)} %slice.25, f32[1,2048]{1,0:T(1,128)S(1)} %copy-done.4, s32[1,2048]{1,0:T(1,128)S(1)} %copy-done), kind=kOutput, calls=%fused_computation.3 | convolution fusion | flops 75507712 | bytes 40960 | tf_op jit(solution)/shard_map/dot_general | solution.py:47
  118.7 0.5 slice.27
  119.2 19.2 %while.10 = (s32[]{:T(128)}, f32[1]{0:T(128)}, f32[1]{0:T(128)}, s32[]{:T(128)}, f32[1]{0:T(128)}) while((s32[]{:T(128)}, f32[1]{0:T(128)}, f32[1]{0:T(128)}, s32[]{:T(128)}, f32[1]{0:T(128)}) %tuple.29), condition=%wide.region_4.5_spmd, body=%wide.region_3.4_spmd.sunk | while | flops 4 | bytes 141 | solution.py:54
  119.8 1.3 collective-permute-start
  121.1 4.5 %collective-permute-done = f32[1]{0:T(128)} collective-permute-done((f32[1]{0:T(128)}, f32[1]{0:T(128)}, u32[]{:S(2)}, u32[]{:S(2)}) %collective-permute-start) | collective-permute-done | bytes 36 | tf_op jit(solution)/shard_map/while/body/eval_jaxpr/ppermute | solution.py:52
  126.8 1.3 collective-permute-start
  128.1 3.6 %collective-permute-done = f32[1]{0:T(128)} collective-permute-done((f32[1]{0:T(128)}, f32[1]{0:T(128)}, u32[]{:S(2)}, u32[]{:S(2)}) %collective-permute-start) | collective-permute-done | bytes 36 | tf_op jit(solution)/shard_map/while/body/eval_jaxpr/ppermute | solution.py:52
  132.9 1.3 collective-permute-start
  134.2 3.6 %collective-permute-done = f32[1]{0:T(128)} collective-permute-done((f32[1]{0:T(128)}, f32[1]{0:T(128)}, u32[]{:S(2)}, u32[]{:S(2)}) %collective-permute-start) | collective-permute-done | bytes 36 | tf_op jit(solution)/shard_map/while/body/eval_jaxpr/ppermute | solution.py:52
  138.4 0.0 copy-done.1
  138.4 1.3 fusion.24
  139.7 2.0 %pad_maximum_fusion = f32[3]{0:T(128)S(1)} fusion(f32[1]{0:T(128)} %bitcast.13, f32[1]{0:T(128)} %bitcast.12, f32[1]{0:T(128)} %bitcast.11), kind=kLoop, calls=%fused_computation.39 | loop fusion | flops 6 | bytes 24 | tf_op jit(solution)/shard_map/stack | solution.py:56
  141.8 24.1 %psum.7 = f32[3]{0:T(128)S(1)} all-reduce(f32[3]{0:T(128)S(1)} %pad_maximum_fusion), channel_id=1, replica_groups=mesh['dp'=2,'cp'=4] {'dp','cp'}, use_global_device_ids=true, to_apply=%region_8.9 | all-reduce | flops 3 | bytes 24 | tf_op jit(solution)/shard_map/psum | solution.py:57
  165.9 0.6 fusion.30
  169.3 0.6 multiply_multiply_fusion
  (7 shorter events, 0.1 us)
Async XLA Ops:
  0.6 9.0 %copy-start.5 = (f32[896]{0:T(1024)S(1)}, f32[896]{0:T(1024)}, u32[]{:S(2)}) copy-start(f32[896]{0:T(1024)} %param.13) | copy-start | bytes 10756
  75.6 26.3 %copy-start.2 = (f32[896]{0:T(1024)S(1)}, f32[896]{0:T(1024)}, u32[]{:S(2)}) copy-start(f32[896]{0:T(1024)} %param.17) | copy-start | bytes 10756
  75.7 26.3 %copy-start.3 = (f32[896]{0:T(1024)S(1)}, f32[896]{0:T(1024)}, u32[]{:S(2)}) copy-start(f32[896]{0:T(1024)} %param.18) | copy-start | bytes 10756
  101.2 6.1 %copy-start = (s32[1,2048]{1,0:T(1,128)S(1)}, s32[1,2048]{1,0:T(1,128)}, u32[]{:S(2)}) copy-start(s32[1,2048]{1,0:T(1,128)} %param.21) | copy-start | bytes 24580
  101.2 10.0 %copy-start.4 = (f32[1,2048]{1,0:T(1,128)S(1)}, f32[1,2048]{1,0:T(1,128)}, u32[]{:S(2)}) copy-start(f32[1,2048]{1,0:T(1,128)} %param.20) | copy-start | bytes 24580
  107.3 31.1 %copy-start.1 = (f32[1,2048]{1,0:T(1,128)}, f32[1,2048]{1,0:T(1,128)S(1)}, u32[]{:S(2)}) copy-start(f32[1,2048]{1,0:T(1,128)S(1)} %convert_multiply_fusion.3) | copy-start | bytes 24580
  107.9 3.4 %collective-permute-start.1 = (f32[1]{0:T(128)}, f32[1]{0:T(128)}, u32[]{:S(2)}, u32[]{:S(2)}) collective-permute-start(f32[1]{0:T(128)} %bitcast.3), channel_id=1, source_target_pairs={{1,0},{2,1},{3,2},{5,4},{6,5},{7,6}} | collective-permute-start | bytes 20 | tf_op jit(solution)/shard_map/ppermute | solution.py:44
  119.8 5.8 %collective-permute-start = (f32[1]{0:T(128)}, f32[1]{0:T(128)}, u32[]{:S(2)}, u32[]{:S(2)}) collective-permute-start(f32[1]{0:T(128)} %add.107), channel_id=1, source_target_pairs={{1,0},{2,1},{3,2},{5,4},{6,5},{7,6}} | collective-permute-start | bytes 20 | tf_op jit(solution)/shard_map/while/body/eval_jaxpr/ppermute | solution.py:52
  126.8 4.9 %collective-permute-start = (f32[1]{0:T(128)}, f32[1]{0:T(128)}, u32[]{:S(2)}, u32[]{:S(2)}) collective-permute-start(f32[1]{0:T(128)} %add.107), channel_id=1, source_target_pairs={{1,0},{2,1},{3,2},{5,4},{6,5},{7,6}} | collective-permute-start | bytes 20 | tf_op jit(solution)/shard_map/while/body/eval_jaxpr/ppermute | solution.py:52
  132.9 4.9 %collective-permute-start = (f32[1]{0:T(128)}, f32[1]{0:T(128)}, u32[]{:S(2)}, u32[]{:S(2)}) collective-permute-start(f32[1]{0:T(128)} %add.107), channel_id=1, source_target_pairs={{1,0},{2,1},{3,2},{5,4},{6,5},{7,6}} | collective-permute-start | bytes 20 | tf_op jit(solution)/shard_map/while/body/eval_jaxpr/ppermute | solution.py:52
where the time goes:
time: 170 us
  matrix products  99.1 us (58%)
  blocking collectives  24.1 us (14%)
  waiting for transfers between devices  13.6 us (8%)
  other arithmetic  12.2 us (7%)
  local copies, waits for them, and re-layouts  7.88 us (5%)
  starting transfers between devices  5.16 us (3%)
  between operations  4.21 us (2%)
  loops' own time  3.68 us (2%)
    dot_general x1, matrix products, critic_values(): jnp.einsum('bsd,df->bsf', normed, w_up, preferred_element_type=jnp.float32)  36.5 us
    dot_general x1, matrix products, critic_values(): jnp.einsum('bsd,df->bsf', normed, w_gate, preferred_element_type=jnp.floa...  29.5 us
    dot_general x1, matrix products, critic_values(): jnp.einsum('bsf,fd->bsd', hidden, w_down, preferred_element_type=jnp.floa...  25.6 us
    psum x1, blocking collectives, local_step(): totals = lax.psum(local_sums, ('dp', 'cp'))  24.1 us
    ppermute x3, waiting for transfers between devices, carry_step(): return lax.ppermute(head_adv + piece_gain * carry, 'cp', left_perm)  11.7 us
    dot_general x1, matrix products, local_step(): jnp.dot(delta, decay_matrix(seq_len), precision=lax.Precision.HIGHEST)  7.45 us
    unnamed x13, local copies, waits for them, and re-layouts  6.16 us
    reduce_sum x1, other arithmetic, critic_values(): return jnp.sum(resid_n * (final_gain * w_value), axis=-1) + b_value  5.36 us
  transfers between devices with their start and end apart: 4, of which 4 were waited for; matrix products, arithmetic and copies ran while one was open for 0% of the time, Pallas kernels for 0%

commit v1 on v0

v1 whole, which is shorter than its diff:
```python
import math
import functools
import jax
import jax.numpy as jnp
from jax import lax
from jax.sharding import PartitionSpec as P
from jax.experimental import pallas as pl
from jax.experimental.pallas import tpu as pltpu

NORM_EPS = 1e-6
WHITEN_EPS = 1e-8
DISCOUNT = 1.0
GAE_LAMBDA = 0.995
LOG_DECAY = math.log(DISCOUNT * GAE_LAMBDA)
DECAY = DISCOUNT * GAE_LAMBDA
LANES = 128
BLOCK = 256
COLS = 512


def chunks(total, step):
    return [(start, min(step, total - start)) for start in range(0, total, step)]


def mlp_kernel(mask_ref, gain_ref, final_ref, wval_ref, bias_ref, x_hbm, wg_hbm, wu_hbm, wd_hbm, out_ref,
               x_v, n_v, u_v, wg_v, wu_v, wd_v, val_v, x_sem, w_sem, d_sem):
    seq, dim = x_hbm.shape
    ffn = wg_v.shape[1]
    cols = chunks(ffn, COLS)

    def up_copies(i):
        c, w = cols[i]
        return (pltpu.make_async_copy(wg_hbm.at[:, pl.ds(c, w)], wg_v.at[:, pl.ds(c, w)], w_sem.at[0, i]),
                pltpu.make_async_copy(wu_hbm.at[:, pl.ds(c, w)], wu_v.at[:, pl.ds(c, w)], w_sem.at[1, i]))

    down_copy = pltpu.make_async_copy(wd_hbm, wd_v, d_sem)

    mask = mask_ref[...]
    rows = lax.broadcasted_iota(jnp.int32, mask.shape, 0)
    lanes = lax.broadcasted_iota(jnp.int32, mask.shape, 1)
    pos = rows * LANES + lanes
    first = jnp.min(jnp.where(mask > 0, pos, seq))
    last = jnp.max(jnp.where(mask > 0, pos, -1))
    first = (first // 16) * 16
    count = jnp.where(last >= 0, (last - first) // BLOCK + 1, 0)

    def start_of(i):
        return pl.multiple_of(jnp.minimum(first + i * BLOCK, seq - BLOCK), 16)

    def x_copy(i):
        slot = lax.rem(i, 2)
        return pltpu.make_async_copy(x_hbm.at[pl.ds(start_of(i), BLOCK), :], x_v.at[slot], x_sem.at[slot])

    def block(i, waits):
        slot = lax.rem(i, 2)
        x_copy(i).wait()

        @pl.when(i + 1 < count)
        def _():
            x_copy(i + 1).start()

        xf = x_v[slot].astype(jnp.float32)
        scale = lax.rsqrt(jnp.mean(xf * xf, axis=-1, keepdims=True) + NORM_EPS)
        n_v[...] = (xf * scale * gain_ref[...]).astype(jnp.bfloat16)
        for j, (c, w) in enumerate(cols):
            if waits:
                for copy in up_copies(j):
                    copy.wait()
            gate = jnp.dot(n_v[...], wg_v[:, c:c + w], preferred_element_type=jnp.float32)
            up = jnp.dot(n_v[...], wu_v[:, c:c + w], preferred_element_type=jnp.float32)
            u_v[:, c:c + w] = (jax.nn.silu(gate) * up).astype(jnp.bfloat16)
        if waits:
            down_copy.wait()
        h = x_v[slot].astype(jnp.float32) + jnp.dot(u_v[...], wd_v[...], preferred_element_type=jnp.float32)
        square = jnp.mean(h * h, axis=-1, keepdims=True)
        proj = jnp.sum(h * (final_ref[...] * wval_ref[...]), axis=-1, keepdims=True)
        val = proj * lax.rsqrt(square + NORM_EPS) + bias_ref[0]
        val_v[pl.ds(start_of(i), BLOCK), :] = jnp.broadcast_to(val, (BLOCK, LANES))

    @pl.when(count > 0)
    def _():
        x_copy(0).start()
        for i in range(len(cols)):
            for copy in up_copies(i):
                copy.start()
        down_copy.start()
        block(0, True)

        @pl.loop(1, count)
        def _(i):
            block(i, False)

    eye = lax.broadcasted_iota(jnp.int32, (LANES, LANES), 0) == lax.broadcasted_iota(jnp.int32, (LANES, LANES), 1)
    for r in range(seq // LANES):
        row = jnp.sum(jnp.where(eye, val_v[r * LANES:(r + 1) * LANES, :], 0.0), axis=0, keepdims=True)
        out_ref[r:r + 1, :] = jnp.where(mask_ref[r:r + 1, :] > 0, row, 0.0)


def mlp_values(mask2, norm_gain, final_gain, w_value, b_value, x, w_gate, w_up, w_down):
    seq, dim = x.shape
    ffn = w_gate.shape[1]
    vmem = pl.BlockSpec(memory_space=pltpu.VMEM)
    hbm = pl.BlockSpec(memory_space=pl.ANY)
    n_cols = len(chunks(ffn, COLS))
    return pl.pallas_call(
        mlp_kernel,
        out_shape=jax.ShapeDtypeStruct((seq // LANES, LANES), jnp.float32),
        in_specs=[vmem, vmem, vmem, vmem, pl.BlockSpec(memory_space=pltpu.SMEM), hbm, hbm, hbm, hbm],
        out_specs=vmem,
        scratch_shapes=[
            pltpu.VMEM((2, BLOCK, dim), jnp.bfloat16),
            pltpu.VMEM((BLOCK, dim), jnp.bfloat16),
            pltpu.VMEM((BLOCK, ffn), jnp.bfloat16),
            pltpu.VMEM((dim, ffn), jnp.bfloat16),
            pltpu.VMEM((dim, ffn), jnp.bfloat16),
            pltpu.VMEM((ffn, dim), jnp.bfloat16),
            pltpu.VMEM((seq, LANES), jnp.float32),
            pltpu.SemaphoreType.DMA((2,)),
            pltpu.SemaphoreType.DMA((2, n_cols)),
            pltpu.SemaphoreType.DMA,
        ],
        compiler_params=pltpu.CompilerParams(vmem_limit_bytes=60 * 1024 * 1024),
        cost_estimate=pl.CostEstimate(flops=6 * seq * dim * ffn, bytes_accessed=3 * 2 * dim * ffn, transcendentals=seq * ffn),
        name="critic_mlp",
    )(mask2, norm_gain[None, :], final_gain[None, :], w_value[None, :], b_value[None], x, w_gate, w_up, w_down)


def tail_kernel(dp_size, cp_size, val_ref, rew_ref, mask_ref, ret_ref, white_ref, send, recv, send_sem, recv_sem):
    n_dev = dp_size * cp_size
    n_rows = val_ref.shape[0]
    seq = n_rows * LANES
    me = lax.axis_index('dp') * cp_size + lax.axis_index('cp')
    barrier = pltpu.get_barrier_semaphore()

    def peer(k):
        other = lax.rem(me + k, n_dev)
        return {'dp': other // cp_size, 'cp': lax.rem(other, cp_size)}

    for k in range(1, n_dev):
        pl.semaphore_signal(barrier, inc=1, device_id=peer(k), device_id_type=pl.DeviceIdType.MESH)

    val = val_ref[...]
    mask = mask_ref[...].astype(jnp.float32)
    rows = lax.broadcasted_iota(jnp.int32, val.shape, 0)
    lanes = lax.broadcasted_iota(jnp.int32, val.shape, 1)
    pos = rows * LANES + lanes

    def up_rows(a, k):
        return jnp.where(rows < n_rows - k, pltpu.roll(a, n_rows - k, 0), 0.0)

    shifted = pltpu.roll(val, LANES - 1, 1)
    next_val = jnp.where(lanes < LANES - 1, shifted, up_rows(shifted, 1))
    adv = mask * rew_ref[...] + DISCOUNT * next_val - val
    k = 1
    while k < LANES:
        adv = adv + DECAY ** k * jnp.where(lanes < LANES - k, pltpu.roll(adv, LANES - k, 1), 0.0)
        k *= 2
    head = jnp.broadcast_to(adv[:, 0:1], adv.shape)
    k = 1
    while k < n_rows:
        head = head + DECAY ** (LANES * k) * up_rows(head, k)
        k *= 2
    adv = adv + jnp.exp((LANES - lanes).astype(jnp.float32) * LOG_DECAY) * up_rows(head, 1)
    reach = jnp.exp((seq - 1 - pos).astype(jnp.float32) * LOG_DECAY)

    m_adv = mask * adv
    m_reach = mask * reach
    at_zero = lanes[0:1] == 0
    parts = [mask, m_adv, m_reach, m_adv * adv, m_adv * reach, m_reach * reach]
    parts = [jnp.sum(a, axis=0, keepdims=True) for a in parts]
    parts += [jnp.where(at_zero, val[0:1], 0.0), jnp.where(at_zero, adv[0:1], 0.0)]
    note = jnp.sum(jnp.concatenate(parts, axis=0), axis=1, keepdims=True)
    note = jnp.broadcast_to(note, (8, LANES))
    send[...] = note
    recv[me] = note

    pl.semaphore_wait(barrier, n_dev - 1)
    copies = []
    for k in range(1, n_dev):
        copies.append(pltpu.make_async_remote_copy(
            src_ref=send, dst_ref=recv.at[me], send_sem=send_sem.at[k], recv_sem=recv_sem.at[k],
            device_id=peer(k), device_id_type=pl.DeviceIdType.MESH))
    for copy in copies:
        copy.start()
    for copy in copies:
        copy.wait()

    zero = jnp.zeros((1, LANES), jnp.float32)
    count, total, square, mine = zero, zero, zero, zero
    for dp in range(dp_size):
        carry = zero
        for cp in reversed(range(cp_size)):
            q = recv[dp * cp_size + cp]
            count = count + q[0:1]
            total = total + q[1:2] + carry * q[2:3]
            square = square + q[3:4] + carry * (2.0 * q[4:5] + carry * q[5:6])
            mine = jnp.where(me == dp * cp_size + cp, carry, mine)
            carry = DISCOUNT * q[6:7] + DECAY * (q[7:8] + DECAY ** (seq - 1) * carry)
    mean = total / count
    inv = lax.rsqrt(square / count - mean * mean + WHITEN_EPS)
    adv = adv + reach * mine
    ret_ref[...] = mask * (adv + val)
    white_ref[...] = mask * (adv - mean) * inv


def tail(dp_size, cp_size, val, rew, mask):
    vmem = pl.BlockSpec(memory_space=pltpu.VMEM)
    shape = jax.ShapeDtypeStruct(val.shape, jnp.float32)
    n_dev = dp_size * cp_size
    return pl.pallas_call(
        functools.partial(tail_kernel, dp_size, cp_size),
        out_shape=(shape, shape),
        in_specs=[vmem] * 3,
        out_specs=(vmem, vmem),
        scratch_shapes=[
            pltpu.VMEM((8, LANES), jnp.float32),
            pltpu.VMEM((n_dev, 8, LANES), jnp.float32),
            pltpu.SemaphoreType.DMA((n_dev,)),
            pltpu.SemaphoreType.DMA((n_dev,)),
        ],
        compiler_params=pltpu.CompilerParams(collective_id=0, has_side_effects=True),
        name="gae_tail",
    )(val, rew, mask)


def solution(mesh):
    dp_size, cp_size = mesh.shape['dp'], mesh.shape['cp']

    def local_step(x_blk, norm_gain, w_gate, w_up, w_down, final_gain, w_value, b_value, rew_blk, mask_blk):
        shape = rew_blk.shape
        fold = (shape[1] // LANES, LANES)
        mask2 = mask_blk.reshape(fold)
        val = mlp_values(mask2, norm_gain, final_gain, w_value, b_value, x_blk[0], w_gate, w_up, w_down)
        ret, white = tail(dp_size, cp_size, val, rew_blk.reshape(fold), mask2)
        return val.reshape(shape), ret.reshape(shape), white.reshape(shape)

    tok_spec = P('dp', 'cp')
    in_specs = (P('dp', 'cp', None), P(None), P(None, None), P(None, None), P(None, None), P(None), P(None), P(), tok_spec, tok_spec)
    return jax.shard_map(local_step, mesh=mesh, in_specs=in_specs, out_specs=(tok_spec, tok_spec, tok_spec), check_vma=False)
```

time: 170 us -> 91.6 us (0.54)
  matrix products: 99.1 us -> 0 us
  Pallas kernels: 0 us -> 83.5 us
  blocking collectives: 24.1 us -> 0 us
  waiting for transfers between devices: 13.6 us -> 0 us
  other arithmetic: 12.2 us -> 0 us
  starting transfers between devices: 5.16 us -> 0 us
  loops' own time: 3.68 us -> 0 us
  between operations: 4.21 us -> 1.3 us
    dot_general x4 -> x0, matrix products: 99.1 us -> none  [the longest x1 36.5 us: critic_values(): jnp.einsum('bsd,df->bsf', normed, w_up, preferred_element_type=jnp.float32)]
    pallas_call x0 -> x2, Pallas kernels: none -> 83.5 us  [the longest x1 81.4 us: tail(): pl.pallas_call(functools.partial(tail_kernel, dp_size, cp_size), out_shap...]
    psum x1 -> x0, blocking collectives: 24.1 us -> none  [local_step(): totals = lax.psum(local_sums, ('dp', 'cp'))]
    ppermute x4 -> x0, waiting for transfers between devices: 13.6 us -> none  [the longest x3 11.7 us: carry_step(): return lax.ppermute(head_adv + piece_gain * carry, 'cp', left_perm)]
    reduce_sum x3 -> x0, other arithmetic: 9.47 us -> none  [the longest x1 5.36 us: critic_values(): return jnp.sum(resid_n * (final_gain * w_value), axis=-1) + b_value]
    ppermute x4 -> x0, starting transfers between devices: 5.16 us -> none  [the longest x3 3.88 us: carry_step(): return lax.ppermute(head_adv + piece_gain * carry, 'cp', left_perm)]
    broadcast_in_dim x0 -> x3, local copies, waits for them, and re-layouts: none -> 3.81 us  [the longest x1 1.27 us: mlp_values(): w_value[None, :]]
    another operation x1 -> x0, loops' own time: 3.68 us -> none  [local_step(): lax.fori_loop(0, cp_size - 1, carry_step, jnp.zeros((row_count,), jnp.flo...]
  transfers between devices with their start and end apart: 4 -> 0, of which waited for: 4 -> 0; matrix products, arithmetic and copies ran while one was open for 0% -> 0% of each run, Pallas kernels for 0% -> 0%
where the time goes in v1:
time: 91.6 us; the launch traced here: 91.2 us
  Pallas kernels  83.5 us (91%)
  local copies, waits for them, and re-layouts  6.4 us (7%)
  between operations  1.3 us (1%)
    pallas_call x1, Pallas kernels, tail(): pl.pallas_call(functools.partial(tail_kernel, dp_size, cp_size), out_shap...  81.4 us
    unnamed x2, local copies, waits for them, and re-layouts  2.59 us
    pallas_call x1, Pallas kernels, mlp_values(): pl.pallas_call(mlp_kernel, out_shape=jax.ShapeDtypeStruct((seq // LANES,...  2.06 us

profile of v1, /device:TPU:0, one launch (start us, length us, event | category | flops | bytes accessed | tf_op | source)
XLA Modules:
  0.0 91.2 jit_solution(13558342752034529235)
XLA Ops:
  1.3 1.3 %broadcast_in_dim.12.gain_ref = f32[1,896]{1,0:T(1,128)} reshape(f32[896]{0:T(1024)} %param.11) | data formatting | bytes 7168 | tf_op jit(solution)/shard_map/broadcast_in_dim | solution.py:125
  2.5 1.3 %broadcast_in_dim.13.final_ref = f32[1,896]{1,0:T(1,128)} reshape(f32[896]{0:T(1024)} %param.15) | data formatting | bytes 7168 | tf_op jit(solution)/shard_map/broadcast_in_dim | solution.py:125
  3.8 1.3 %broadcast_in_dim.14.wval_ref = f32[1,896]{1,0:T(1,128)} reshape(f32[896]{0:T(1024)} %param.16) | data formatting | bytes 7168 | tf_op jit(solution)/shard_map/broadcast_in_dim | solution.py:125
  5.1 2.1 %critic_mlp.1.val_ref = f32[16,128]{1,0:T(8,128)} custom-call(s32[16,128]{1,0:T(8,128)} %bitcast.8, f32[1,896]{1,0:T(1,128)} %broadcast_in_dim.12.gain_ref, f32[1,896]{1,0:T(1,128)} %broadcast_in_dim.13.final_ref, f32[1,896]{1,0:T(1,128)} %broadcast_in_dim.14.wval_ref, f32[1]{0:T(128)} %bitcast.7.bias_ref, bf16[2048,896]{1,0:T(8,128)(2,1)} %bitcast.14, ...), custom_call_target="tpu_custom_call" | custom-call | flops 53552873472 | bytes 26148864 | tf_op jit(solution)/shard_map/critic_mlp/pallas_call | solution.py:105
  7.2 81.4 %gae_tail.1 = (f32[16,128]{1,0:T(8,128)}, f32[16,128]{1,0:T(8,128)}) custom-call(f32[16,128]{1,0:T(8,128)} %critic_mlp.1.val_ref, f32[16,128]{1,0:T(8,128)} %bitcast.10, s32[16,128]{1,0:T(8,128)} %bitcast.9), custom_call_target="tpu_custom_call" | custom-call | tf_op jit(solution)/shard_map/gae_tail/pallas_call | solution.py:210
  88.6 1.3 %copy.16 = f32[1,2048]{1,0:T(1,128)} copy(f32[1,2048]{1,0:T(1,128)} %bitcast.13) | data formatting | bytes 16384
  89.9 1.3 %copy.17 = f32[1,2048]{1,0:T(1,128)} copy(f32[1,2048]{1,0:T(1,128)} %bitcast.12) | data formatting | bytes 16384
